TPU v7x, 32 devices: a 4x4x1 block of a 4x4x8 slice. The times are simulated.
32 devices in a mesh: data: 1 (over z), col: 4 (over y), row: 8 (over x, core).
Axes of the slice: x: 4, y: 4, z: 1, core: 2. Of those that a mesh axis runs over, the one named last changes fastest.
The devices are a block of a 4x4x8 slice.
Arguments:
- tokens: bfloat16 [4096, 8192], P(('data', 'row'), 'col')
- w_qkv: bfloat16 [8192, 10240], P('row', 'col')
- w_out: bfloat16 [8192, 8192], P('row', 'col')
- doc_ids: int32 [4096], P(('data', 'row'))
Outputs:
- output: bfloat16 [4096, 8192], P(('data', 'row'), 'col')
All inputs are finite; a program needn't handle non-finite values.
Results may differ from a plain program's by a relative error of at most 0.00445.
Values are sent between devices in bfloat16 or wider.
A program may use at most 768 MiB of HBM per device.

v0:
```python
import functools

import jax
import jax.numpy as jnp
from jax import lax
from jax.experimental import pallas as pl
from jax.experimental.pallas import tpu as pltpu
from jax.sharding import PartitionSpec as P

HEAD_DIM = 128
CORES = 2
Q_TILE = 256
CHUNKS = 4
LOG2E = 1.4426950408889634
BOTH = (0, 1)
YES, NO = True, False


MESH = pl.DeviceIdType.MESH


def near_x(x):
    return x + 1 - 2 * (x % 2)


def qkv_kernel(n_x, n_y, tok_ref, w_ref, wo_ref, seg_ref, q_ref, kv_ref, segs_ref, got_ref, xg, wg, acc, w_send, w_recv, d_send, d_recv, t_send, t_recv, y_send, y_recv, k_send, k_recv, l_sem, s_send, s_recv, o_send, o_recv):
    r, y = lax.axis_index("row"), lax.axis_index("col")
    x, c = r // CORES, r % CORES
    xn, xf = near_x(x), n_x - 1 - x
    xnf = n_x - 1 - xn
    half = x // (n_x // 2)
    before, after, across = (y + n_y - 1) % n_y, (y + 1) % n_y, (y + 2) % n_y
    rows, width = tok_ref.shape
    depth = w_ref.shape[0]
    part = w_ref.shape[1] // 2
    ctx = part - 2 * HEAD_DIM
    mid, cut, quarter = rows // 2, depth // 2, rows // 4
    near, far, core = {"row": CORES * xn + c}, {"row": CORES * xf + c}, {"row": CORES * x + 1 - c}
    up, down = {"col": after}, {"col": before}

    barrier = pltpu.get_barrier_semaphore()
    n_row = CORES * n_x
    row_peers = [{"row": (r + d) % n_row} for d in range(1, n_row)]
    for peer in row_peers + [up, down]:
        pl.semaphore_signal(barrier, inc=1, device_id=peer, device_id_type=MESH)
    pl.semaphore_wait(barrier, n_row + 1)

    started = []

    def send(src, dst, s_sem, r_sem, peer):
        copy = pltpu.make_async_remote_copy(src_ref=src, dst_ref=dst, send_sem=s_sem, recv_sem=r_sem, device_id=peer, device_id_type=MESH)
        copy.start()
        started.append(copy)
        return copy

    mine = pl.ds(pl.multiple_of(half * part, 128), part)
    theirs = pl.ds(pl.multiple_of((1 - half) * part, 128), part)

    def w_slot(chip, plane, i):
        return wg.at[chip, pl.ds(pl.multiple_of(plane * depth + i * cut, cut), cut), :]

    def send_w(kind, i):
        src_rows = pl.ds(i * cut, cut)
        if kind == 0:
            return send(w_ref.at[src_rows, mine], w_slot(x, c, i), w_send.at[0, i], w_recv.at[0, i], near)
        if kind == 1:
            return send(w_ref.at[src_rows, theirs], w_slot(x, c, i), w_send.at[1, i], w_recv.at[1, i], far)
        return send(w_slot(xf, c, i), w_slot(xf, c, i), w_send.at[2, i], w_recv.at[2, i], near)

    def share(chip, i, at):
        src = w_ref.at[pl.ds(i * cut, cut), mine] if at == 0 else w_slot(chip, c, i)
        return send(src, w_slot(chip, c, i), d_send.at[at, i], d_recv.at[at, i], core)

    def x_slot(b, at, lo, n):
        return xg.at[b, at, pl.ds(lo, n), :]

    def send_t(a):
        return send(tok_ref.at[pl.ds(a * mid, mid), :], x_slot(1, y, a * mid, mid), t_send.at[a], t_recv.at[a], far)

    def send_y(b, a, way):
        src = tok_ref.at[pl.ds(a * mid, mid), :] if b == 0 else x_slot(1, y, a * mid, mid)
        return send(src, x_slot(b, y, a * mid, mid), y_send.at[b, a, way], y_recv.at[b, a, way], (up, down)[way])

    def pass_y(b, a, way):
        at = (before, after)[way]
        piece = x_slot(b, at, a * mid + way * quarter, quarter)
        return send(piece, piece, y_send.at[b, a, 2 + way], y_recv.at[b, a, 2 + way], (up, down)[way])

    segs = [send(seg_ref, segs_ref.at[r], s_send.at[d], s_recv.at[d], peer) for d, peer in enumerate(row_peers)]
    w_far = [send_w(1, 0)]
    y_own = [[send_y(0, a, way) for way in BOTH] for a in BOTH]
    w_near = [send_w(0, 0)]
    tok = [send_t(0)]
    w_near.append(send_w(0, 1))
    w_far.append(send_w(1, 1))
    tok.append(send_t(1))
    chunk = depth // CHUNKS
    wo_got = [send(wo_ref.at[pl.ds(i * chunk, chunk), :], got_ref.at[1 + i], o_send.at[1 + i], o_recv.at[1 + i], far) for i in BOTH]
    locals_ = [
        pltpu.make_async_copy(seg_ref, segs_ref.at[r], l_sem.at[2]),
        pltpu.make_async_copy(tok_ref, xg.at[0, y], l_sem.at[0]),
        pltpu.make_async_copy(w_ref.at[:, mine], wg.at[x, pl.ds(pl.multiple_of(c * depth, depth), depth), :], l_sem.at[1]),
    ]
    for copy in locals_:
        copy.start()
    d_own = [share(x, i, 0) for i in BOTH]

    def multiply(b, lo, n, chip, first, last):
        tile = 2 * HEAD_DIM

        @pl.loop(0, part // tile)
        def _(j):
            cols = pl.ds(pl.multiple_of(j * tile, tile), tile)
            dot = jnp.dot(xg[b, chip, pl.ds(lo, n), :], wg[chip, :, cols], preferred_element_type=jnp.float32)
            if not first:
                dot = dot + acc[pl.ds(lo, n), cols]
            if not last:
                acc[pl.ds(lo, n), cols] = dot
            else:
                out = dot.astype(jnp.bfloat16)

                @pl.when(j < ctx // tile)
                def _():
                    q_ref[pl.ds(b * rows + lo, n), cols] = out

                @pl.when(j == ctx // tile)
                def _():
                    kv_ref[pl.ds(b * rows + lo, n), :] = out

    def kv_slot(s):
        return kv_ref.at[pl.ds(s * rows, rows), :]

    def kv_near(b):
        return send(kv_slot(b), kv_slot(2 + b), k_send.at[b], k_recv.at[b], near)

    def kv_core(s):
        return send(kv_slot(s), kv_slot(4 + s), k_send.at[2 + s], k_recv.at[2 + s], core)

    def relay(b, a):
        got = []
        for way in BOTH:
            (y_own if b == 0 else y_par)[a][way].wait_recv()
            got.append(pass_y(b, a, way))
        return got

    y_far = [relay(0, 0)]
    w_far[0].wait_recv()
    w_nf = [send_w(2, 0)]
    d_far = [share(xf, 0, 2)]
    w_near[0].wait_recv()
    d_near = [share(xn, 0, 1)]
    y_far.append(relay(0, 1))
    tok[0].wait_recv()
    y_par = [[send_y(1, 0, way) for way in BOTH]]
    w_near[1].wait_recv()
    d_near.append(share(xn, 1, 1))
    for pair in y_far:
        for copy in pair:
            copy.wait_recv()
    for copy in locals_:
        copy.wait()
    for copy in d_own:
        copy.wait_recv()
    multiply(0, 0, rows, x, YES, NO)
    for copy in d_near:
        copy.wait_recv()
    w_far[1].wait_recv()
    w_nf.append(send_w(2, 1))
    wo_got.append(send(wo_ref.at[pl.ds(0, chunk), :], got_ref.at[0], o_send.at[0], o_recv.at[0], near))
    d_far.append(share(xf, 1, 2))
    multiply(0, 0, rows, xn, NO, NO)
    w_nf[0].wait_recv()
    d_nf = [share(xnf, 0, 3)]
    y_pfar = [relay(1, 0)]
    tok[1].wait_recv()
    y_par.append([send_y(1, 1, way) for way in BOTH])
    for copy in d_far:
        copy.wait_recv()
    multiply(0, 0, rows, xf, NO, NO)
    w_nf[1].wait_recv()
    d_nf.append(share(xnf, 1, 3))
    for copy in d_nf:
        copy.wait_recv()
    multiply(0, 0, rows, xnf, NO, YES)
    for copy in y_pfar[0]:
        copy.wait_recv()
    multiply(1, 0, mid, y, YES, NO)
    k_near, k_core = [kv_near(0)], [kv_core(0)]
    multiply(1, 0, mid, before, NO, NO)
    y_pfar.append(relay(1, 1))
    multiply(1, 0, mid, after, NO, NO)
    multiply(1, 0, mid, across, NO, YES)
    multiply(1, mid, mid, y, YES, NO)
    multiply(1, mid, mid, before, NO, NO)
    multiply(1, mid, mid, after, NO, NO)
    k_near[0].wait_recv()
    k_core.append(kv_core(2))
    for copy in y_pfar[1]:
        copy.wait_recv()
    multiply(1, mid, mid, across, NO, YES)
    k_near.append(kv_near(1))
    k_core.append(kv_core(1))
    k_near[1].wait_recv()
    k_core.append(kv_core(3))
    for copy in k_core + wo_got + segs:
        copy.wait_recv()
    for copy in started:
        copy.wait_send()


def project_qkv(tokens, w_qkv, w_out, doc_ids, n_x, n_y):
    rows, width = tokens.shape
    depth, cols = w_qkv.shape
    part = cols // 2
    ctx = part - 2 * HEAD_DIM
    n_row = CORES * n_x
    dma = pltpu.SemaphoreType.DMA
    anywhere, vmem = pl.BlockSpec(memory_space=pl.ANY), pl.BlockSpec(memory_space=pltpu.VMEM)
    segs = doc_ids.reshape(rows // 128, 128)
    return pl.pallas_call(
        functools.partial(qkv_kernel, n_x, n_y),
        out_shape=(
            jax.ShapeDtypeStruct((2 * rows, ctx), jnp.bfloat16),
            jax.ShapeDtypeStruct((n_row * rows, 2 * HEAD_DIM), jnp.bfloat16),
            jax.ShapeDtypeStruct((n_row,) + segs.shape, jnp.int32),
            jax.ShapeDtypeStruct((3, depth // CHUNKS, w_out.shape[1]), jnp.bfloat16),
        ),
        in_specs=[anywhere] * 4,
        out_specs=(vmem, vmem, vmem, anywhere),
        scratch_shapes=[
            pltpu.VMEM((2, n_y, rows, width), jnp.bfloat16),
            pltpu.VMEM((n_x, CORES * depth, part), jnp.bfloat16),
            pltpu.VMEM((rows, part), jnp.float32),
            dma((3, 2)), dma((3, 2)), dma((4, 2)), dma((4, 2)), dma((2,)), dma((2,)),
            dma((2, 2, 4)), dma((2, 2, 4)), dma((6,)), dma((6,)), dma((3,)),
            dma((n_row - 1,)), dma((n_row - 1,)), dma((3,)), dma((3,)),
        ],
        compiler_params=pltpu.CompilerParams(collective_id=0, has_side_effects=YES, vmem_limit_bytes=60 * 1024 * 1024),
        cost_estimate=pl.CostEstimate(flops=4 * rows * n_y * width * part, bytes_accessed=2 * depth * cols, transcendentals=0),
        name="project_qkv",
    )(tokens, w_qkv, w_out, segs)


def attend_kernel(n_x, n_y, q_ref, kv_ref, segs_ref, got_ref, w_ref, out_ref, wo, panel, obuf, sbuf, segq, mbuf, lbuf, abuf, n_send, n_recv, f_send, f_recv, d_send, d_recv, t_send, t_recv, y_send, y_recv, l_sem):
    r, y = lax.axis_index("row"), lax.axis_index("col")
    x, c = r // CORES, r % CORES
    xn, xf = near_x(x), n_x - 1 - x
    xnf = n_x - 1 - xn
    half = x // (n_x // 2)
    before, after, across = (y + n_y - 1) % n_y, (y + 1) % n_y, (y + 2) % n_y
    rows = out_ref.shape[0]
    keys = kv_ref.shape[0]
    chunk = w_ref.shape[0] // CHUNKS
    width = w_ref.shape[1]
    heads = q_ref.shape[1] // HEAD_DIM
    tiles = 2 * rows // Q_TILE
    units = tiles * heads
    eighth = Q_TILE // 2
    coef = HEAD_DIM ** -0.5 * LOG2E
    lowest = jnp.finfo(jnp.float32).min
    near, far, core = {"row": CORES * xn + c}, {"row": CORES * xf + c}, {"row": CORES * x + 1 - c}
    up, down = {"col": after}, {"col": before}

    barrier = pltpu.get_barrier_semaphore()
    for peer in (near, far, core, up, down):
        pl.semaphore_signal(barrier, inc=1, device_id=peer, device_id_type=MESH)
    pl.semaphore_wait(barrier, 5)

    started = []

    def send(src, dst, s_sem, r_sem, peer):
        copy = pltpu.make_async_remote_copy(src_ref=src, dst_ref=dst, send_sem=s_sem, recv_sem=r_sem, device_id=peer, device_id_type=MESH)
        copy.start()
        started.append(copy)
        return copy

    def w_slot(k, chip):
        return wo.at[k, pl.ds(pl.multiple_of((CORES * chip + c) * chunk, chunk), chunk), :]

    def w_mine(k):
        return w_ref.at[pl.ds(k * chunk, chunk), :]

    def share(k, origin, src=None):
        slot = w_slot(k, (x, xn, xf, xnf)[origin])
        return send(slot if src is None else src, slot, d_send.at[k, origin], d_recv.at[k, origin], core)

    def to_near(k, src, chip):
        return send(src, w_slot(k, chip), n_send.at[k, 0], n_recv.at[k, 0], near)

    def to_far(k, src, chip):
        return send(src, w_slot(k, chip), f_send.at[k, 0], f_recv.at[k, 0], far)

    direct = {2: to_near(2, w_mine(2), x), 3: to_near(3, w_mine(3), x)}
    straight = {2: to_far(2, w_mine(2), x), 3: to_far(3, w_mine(3), x)}
    direct[1] = to_near(1, w_mine(1), x)
    corner = {0: send(got_ref.at[1], w_slot(0, xf), n_send.at[0, 1], n_recv.at[0, 1], near)}
    corner[1] = send(got_ref.at[2], w_slot(1, xf), n_send.at[1, 1], n_recv.at[1, 1], near)
    places = [(w_mine(k), w_slot(k, x)) for k in range(CHUNKS)]
    places += [(got_ref.at[0], w_slot(0, xn)), (got_ref.at[1], w_slot(0, xf)), (got_ref.at[2], w_slot(1, xf))]
    placed = [pltpu.make_async_copy(src, dst, l_sem.at[i]) for i, (src, dst) in enumerate(places)]
    for copy in placed:
        copy.start()
    shared = [share(k, 0, w_mine(k)) for k in range(CHUNKS)]
    shared += [share(0, 1, got_ref.at[0]), share(0, 2, got_ref.at[1]), share(1, 2, got_ref.at[2])]

    for i in range(2 * rows // 128):
        at = r if i < rows // 128 else CORES * xf + c
        line = segs_ref[at, pl.ds(i % (rows // 128), 1), :].astype(jnp.float32)
        segq[pl.ds(i * 128, 128), :] = jnp.broadcast_to(line, (128, 128)).T

    def key_row(j):
        odd, fam, plane = j % 2, (j // 2) % 2, j // 4
        base = x + fam * (xn - x)
        chip = base + odd * (n_x - 1 - 2 * base)
        return CORES * chip + c + plane * (1 - 2 * c)

    blocks = keys // rows
    lanes = rows // 128

    def scores(u, j):
        b, tile, h = u % 3, u // heads, u % heads
        q = q_ref[pl.ds(pl.multiple_of(tile * Q_TILE, Q_TILE), Q_TILE), pl.ds(pl.multiple_of(h * HEAD_DIM, HEAD_DIM), HEAD_DIM)]
        k = kv_ref[pl.ds(pl.multiple_of(j * rows, rows), rows), pl.ds(0, HEAD_DIM)]
        s = lax.dot_general(q, k, (((1,), (1,)), ((), ())), preferred_element_type=jnp.float32)
        own = segq[pl.ds(pl.multiple_of(tile * Q_TILE, Q_TILE), Q_TILE), :]
        seg = segs_ref[key_row(j)].astype(jnp.float32)
        top = mbuf[b]
        for i in range(lanes):
            part = jnp.where(own == seg[i:i + 1, :], s[:, i * 128:(i + 1) * 128], lowest)
            sbuf[b, j * lanes + i] = part
            top = jnp.maximum(top, part)
        mbuf[b] = top

    def powers(u, j):
        b = u % 3
        top = mbuf[b]
        total = lbuf[b]
        for i in range(lanes):
            e = jnp.exp2((sbuf[b, j * lanes + i] - top) * coef)
            sbuf[b, j * lanes + i] = e
            total = total + e
        lbuf[b] = total

    def context(u, j):
        b = u % 3
        inv = lbuf[b]
        p = jnp.concatenate([(sbuf[b, j * lanes + i] * inv).astype(jnp.bfloat16) for i in range(lanes)], axis=1)
        v = kv_ref[pl.ds(pl.multiple_of(j * rows, rows), rows), pl.ds(HEAD_DIM, HEAD_DIM)]
        abuf[...] += jnp.dot(p, v, preferred_element_type=jnp.float32)

    def open_unit(u, a, b, e):
        if a:
            mbuf[u % 3] = jnp.full(mbuf.shape[1:], lowest, jnp.float32)
        if b:
            lbuf[(u - 1) % 3] = jnp.zeros(lbuf.shape[1:], jnp.float32)
        if e:
            abuf[...] = jnp.zeros(abuf.shape, jnp.float32)

    def close_unit(u, a, b, e):
        if a:
            mbuf[u % 3] = jnp.broadcast_to(jnp.max(mbuf[u % 3], axis=1, keepdims=YES), mbuf.shape[1:])
        if b:
            lbuf[(u - 1) % 3] = 1.0 / jnp.broadcast_to(jnp.sum(lbuf[(u - 1) % 3], axis=1, keepdims=YES), lbuf.shape[1:])
        if e:
            tile, h = (u - 2) // heads, (u - 2) % heads
            out = abuf[...].astype(jnp.bfloat16)
            per = heads // CHUNKS
            lo = pl.multiple_of((h % per) * HEAD_DIM, HEAD_DIM)
            mine = pl.multiple_of((CORES * y + half) * chunk, chunk)

            @pl.when(tile < tiles // 2)
            def _():
                panel[h // per, pl.ds(pl.multiple_of(tile * Q_TILE, Q_TILE), Q_TILE), pl.ds(pl.multiple_of(mine + lo, HEAD_DIM), HEAD_DIM)] = out

            @pl.when(tile >= tiles // 2)
            def _():
                obuf[h // per, pl.ds(pl.multiple_of((tile - tiles // 2) * Q_TILE, Q_TILE), Q_TILE), pl.ds(lo, HEAD_DIM)] = out

    def unit(u, a, b, e):
        open_unit(u, a, b, e)

        @pl.loop(0, blocks)
        def _(j):
            if a:
                scores(u, j)
            if b:
                powers(u - 1, j)
            if e:
                context(u - 2, j)

        close_unit(u, a, b, e)

    def o_slot(yy, f, lo, n):
        hh = half + f * (1 - 2 * half)
        return panel.at[:, pl.ds(lo, n), pl.ds(pl.multiple_of((CORES * yy + hh) * chunk, chunk), chunk)]

    def send_o(a):
        return pltpu.make_async_remote_copy(
            src_ref=obuf.at[:, pl.ds(a * Q_TILE, Q_TILE), :], dst_ref=o_slot(y, 0, a * Q_TILE, Q_TILE),
            send_sem=t_send.at[a], recv_sem=t_recv.at[a], device_id=far, device_id_type=MESH)

    def y_copy(f, a, way):
        piece = o_slot(y, f, a * Q_TILE, Q_TILE)
        return pltpu.make_async_remote_copy(src_ref=piece, dst_ref=piece, send_sem=y_send.at[f, a, way], recv_sem=y_recv.at[f, a, way], device_id=(up, down)[way], device_id_type=MESH)

    def y_pass(f, a, way):
        piece = o_slot((before, after)[way], f, a * Q_TILE + way * eighth, eighth)
        return pltpu.make_async_remote_copy(src_ref=piece, dst_ref=piece, send_sem=y_send.at[f, a, 2 + way], recv_sem=y_recv.at[f, a, 2 + way], device_id=(up, down)[way], device_id_type=MESH)

    def w_copy(kind, k):
        if kind == 0:
            return pltpu.make_async_remote_copy(src_ref=w_slot(k, xn), dst_ref=w_slot(k, xn), send_sem=f_send.at[k, 1], recv_sem=f_recv.at[k, 1], device_id=far, device_id_type=MESH)
        slot = w_slot(k, (x, xn, xf, xnf)[kind])
        return pltpu.make_async_remote_copy(src_ref=slot, dst_ref=slot, send_sem=d_send.at[k, kind], recv_sem=d_recv.at[k, kind], device_id=core, device_id_type=MESH)

    def near_in(k):
        direct[k].wait_recv()
        if k >= 2:
            w_copy(0, k).start()
        w_copy(1, k).start()

    def far_in(k):
        straight[k].wait_recv()
        w_copy(2, k).start()

    def corner_in(k):
        (corner[k] if k < 2 else w_copy(0, k)).wait_recv()
        w_copy(3, k).start()

    def y_start(f, a):
        for way in BOTH:
            y_copy(f, a, way).start()

    def y_relay(f, a):
        for way in BOTH:
            y_copy(f, a, way).wait_recv()
            y_pass(f, a, way).start()

    def o_in(a):
        send_o(a).wait_recv()
        y_start(1, a)

    events = {
        heads + 3: [lambda: y_start(0, 0), lambda: near_in(2), lambda: far_in(2)],
        2 * heads + 3: [lambda: y_start(0, 1), lambda: y_relay(0, 0)],
        2 * heads + 6: [lambda: near_in(3), lambda: far_in(3)],
        3 * heads + 1: [lambda: y_relay(0, 1)],
        3 * heads + 3: [lambda: send_o(0).start()],
        4 * heads - 1: [lambda: corner_in(2)],
    }

    unit(0, YES, NO, NO)
    unit(1, YES, YES, NO)

    @pl.loop(2, units)
    def _(u):
        for at, steps in events.items():
            @pl.when(u == at)
            def _(steps=steps):
                for step in steps:
                    step()
        unit(u, YES, YES, YES)

    unit(units, NO, YES, YES)
    unit(units + 1, NO, NO, YES)

    def multiply(a, k, first, last):
        tile = 2 * HEAD_DIM

        @pl.loop(0, width // tile)
        def _(n):
            cols = pl.ds(pl.multiple_of(n * tile, tile), tile)
            dot = jnp.dot(panel[k, pl.ds(a * Q_TILE, Q_TILE), :], wo[k, :, cols], preferred_element_type=jnp.float32)
            per = tile // 128
            if not first:
                dot = dot + jnp.concatenate([sbuf[a, n * per + i] for i in range(per)], axis=1)
            if not last:
                for i in range(per):
                    sbuf[a, n * per + i] = dot[:, i * 128:(i + 1) * 128]
            else:
                out_ref[pl.ds(a * Q_TILE, Q_TILE), cols] = dot.astype(jnp.bfloat16)

    o_in(0)
    send_o(1).start()
    corner_in(0)
    near_in(1)
    y_relay(1, 0)
    o_in(1)
    for f in BOTH:
        for way in BOTH:
            y_pass(f, 0, way).wait_recv()
    for copy in placed:
        copy.wait()
    for copy in shared:
        copy.wait_recv()
    for kind in (1, 2, 3):
        w_copy(kind, 2).wait_recv()
    multiply(0, 2, YES, NO)
    corner_in(3)
    y_relay(1, 1)
    w_copy(3, 0).wait_recv()
    multiply(0, 0, NO, NO)
    for kind in (1, 2, 3):
        w_copy(kind, 3).wait_recv()
    multiply(0, 3, NO, NO)
    for f in BOTH:
        for way in BOTH:
            y_pass(f, 1, way).wait_recv()
    multiply(1, 2, YES, NO)
    corner_in(1)
    multiply(1, 0, NO, NO)
    multiply(1, 3, NO, NO)
    w_copy(1, 1).wait_recv()
    w_copy(3, 1).wait_recv()
    multiply(0, 1, NO, YES)
    multiply(1, 1, NO, YES)
    for copy in started:
        copy.wait_send()
    for k in (2, 3):
        w_copy(0, k).wait_send()
        for kind in (1, 2, 3):
            w_copy(kind, k).wait_send()
    for kind, k in ((3, 0), (1, 1), (3, 1)):
        w_copy(kind, k).wait_send()
    for a in BOTH:
        send_o(a).wait_send()
        for f in BOTH:
            for way in BOTH:
                y_copy(f, a, way).wait_send()
                y_pass(f, a, way).wait_send()


def attend_project(q, kv, segs, got, w_out, n_x, n_y):
    rows, ctx = q.shape[0] // 2, q.shape[1]
    keys = kv.shape[0]
    depth, width = w_out.shape
    n_row = CORES * n_x
    chunk = depth // CHUNKS
    dma = pltpu.SemaphoreType.DMA
    anywhere, vmem = pl.BlockSpec(memory_space=pl.ANY), pl.BlockSpec(memory_space=pltpu.VMEM)
    return pl.pallas_call(
        functools.partial(attend_kernel, n_x, n_y),
        out_shape=jax.ShapeDtypeStruct((rows, width), jnp.bfloat16),
        in_specs=[vmem, vmem, vmem, anywhere, anywhere],
        out_specs=vmem,
        scratch_shapes=[
            pltpu.VMEM((CHUNKS, n_row * chunk, width), jnp.bfloat16),
            pltpu.VMEM((CHUNKS, rows, n_row * chunk), jnp.bfloat16),
            pltpu.VMEM((CHUNKS, rows, chunk), jnp.bfloat16),
            pltpu.VMEM((3, keys // 128, Q_TILE, 128), jnp.float32),
            pltpu.VMEM((2 * rows, 128), jnp.float32),
            pltpu.VMEM((3, Q_TILE, 128), jnp.float32),
            pltpu.VMEM((3, Q_TILE, 128), jnp.float32),
            pltpu.VMEM((Q_TILE, HEAD_DIM), jnp.float32),
            dma((CHUNKS, 2)), dma((CHUNKS, 2)), dma((CHUNKS, 2)), dma((CHUNKS, 2)),
            dma((CHUNKS, 4)), dma((CHUNKS, 4)), dma((2,)), dma((2,)),
            dma((2, 2, 4)), dma((2, 2, 4)), dma((CHUNKS + 3,)),
        ],
        compiler_params=pltpu.CompilerParams(collective_id=1, has_side_effects=YES, vmem_limit_bytes=63 * 1024 * 1024),
        cost_estimate=pl.CostEstimate(flops=8 * rows * ctx * keys, bytes_accessed=4 * depth * width, transcendentals=0),
        name="attend_project",
    )(q, kv, segs, got, w_out)


def solution(mesh):
    n_x, n_y = mesh.shape["row"] // CORES, mesh.shape["col"]

    def local_block(tokens, w_qkv, w_out, doc_ids):
        q, kv, segs, got = project_qkv(tokens, w_qkv, w_out, doc_ids, n_x, n_y)
        return attend_project(q, kv, segs, got, w_out, n_x, n_y)

    row_spec = P(("data", "row"), "col")
    weight_spec = P("row", "col")
    return jax.shard_map(local_block, mesh=mesh, in_specs=(row_spec, weight_spec, weight_spec, P(("data", "row"))), out_specs=row_spec, check_vma=NO)
```

profile of v0, /device:TPU:97, one launch (start us, length us, event | category | flops | bytes accessed | tf_op | source)
XLA Modules:
  0.0 372.4 jit_solution(7875481890724497573)
XLA Ops:
  0.0 161.2 %project_qkv.1 = (bf16[1024,1024]{1,0:T(8,128)(2,1)}, bf16[4096,256]{1,0:T(8,128)(2,1)}, s32[8,4,128]{2,1,0:T(4,128)}, bf16[3,256,2048]{2,1,0:T(8,128)(2,1)}) custom-call(bf16[512,2048]{1,0:T(8,128)(2,1)} %tok_ref.1, bf16[1024,2560]{1,0:T(8,128)(2,1)} %w_ref.2, bf16[1024,2048]{1,0:T(8,128)(2,1)} %w_ref.3, s32[4,128]{1,0:T(4,128)} %bitcast.1), custom_call_target="tpu_custom_call" | custom-call | flops 21474836480 | bytes 5242880 | tf_op jit(solution)/shard_map/project_qkv/pallas_call | solution.py:220
  161.2 208.1 %attend_project.1 = bf16[512,2048]{1,0:T(8,128)(2,1)} custom-call(bf16[1024,1024]{1,0:T(8,128)(2,1)} %get-tuple-element.9.q_ref, bf16[4096,256]{1,0:T(8,128)(2,1)} %get-tuple-element.10.kv_ref, s32[8,4,128]{2,1,0:T(4,128)} %get-tuple-element.11.segs_ref, bf16[3,256,2048]{2,1,0:T(8,128)(2,1)} %get-tuple-element.12.got_ref, bf16[1024,2048]{1,0:T(8,128)(2,1)} %w_ref.3), custom_call_target="tpu_custom_call" | custom-call | flops 17179869184 | bytes 8388608 | tf_op jit(solution)/shard_map/attend_project/pallas_call | solution.py:541
  369.3 3.2 copy.6
where the time goes:
time: 373 us; the launch traced here: 372 us
  Pallas kernels  369 us (99%)
    pallas_call x1, Pallas kernels, attend_project(): pl.pallas_call(functools.partial(attend_kernel, n_x, n_y), out_shape=jax....  208 us
    pallas_call x1, Pallas kernels, project_qkv(): pl.pallas_call(functools.partial(qkv_kernel, n_x, n_y), out_shape=(jax.Sh...  161 us

commit v1 on v0

--- a/solution.py
+++ b/solution.py
@@ -11,6 +11,7 @@
 CORES = 2
 Q_TILE = 256
 CHUNKS = 4
+UNROLL = 2
 LOG2E = 1.4426950408889634
 BOTH = (0, 1)
 YES, NO = True, False
@@ -318,7 +319,7 @@
     lanes = rows // 128
 
     def scores(u, j):
-        b, tile, h = u % 3, u // heads, u % heads
+        b, tile, h = u % 3, (u // heads + tiles // 2) % tiles, u % heads
         q = q_ref[pl.ds(pl.multiple_of(tile * Q_TILE, Q_TILE), Q_TILE), pl.ds(pl.multiple_of(h * HEAD_DIM, HEAD_DIM), HEAD_DIM)]
         k = kv_ref[pl.ds(pl.multiple_of(j * rows, rows), rows), pl.ds(0, HEAD_DIM)]
         s = lax.dot_general(q, k, (((1,), (1,)), ((), ())), preferred_element_type=jnp.float32)
@@ -368,44 +369,50 @@
             lo = pl.multiple_of((h % per) * HEAD_DIM, HEAD_DIM)
             mine = pl.multiple_of((CORES * y + half) * chunk, chunk)
 
+            at = pl.ds(pl.multiple_of(tile % (tiles // 2) * Q_TILE, Q_TILE), Q_TILE)
+
+            @pl.when(tile >= tiles // 2)
+            def _():
+                panel[h // per, at, pl.ds(pl.multiple_of(mine + lo, HEAD_DIM), HEAD_DIM)] = out
+
             @pl.when(tile < tiles // 2)
             def _():
-                panel[h // per, pl.ds(pl.multiple_of(tile * Q_TILE, Q_TILE), Q_TILE), pl.ds(pl.multiple_of(mine + lo, HEAD_DIM), HEAD_DIM)] = out
-
-            @pl.when(tile >= tiles // 2)
-            def _():
-                obuf[h // per, pl.ds(pl.multiple_of((tile - tiles // 2) * Q_TILE, Q_TILE), Q_TILE), pl.ds(lo, HEAD_DIM)] = out
+                obuf[h // per, at, pl.ds(lo, HEAD_DIM)] = out
 
     def unit(u, a, b, e):
         open_unit(u, a, b, e)
 
-        @pl.loop(0, blocks)
-        def _(j):
-            if a:
-                scores(u, j)
-            if b:
-                powers(u - 1, j)
-            if e:
-                context(u - 2, j)
+        @pl.loop(0, blocks // UNROLL)
+        def _(jj):
+            for i in range(UNROLL):
+                j = jj * UNROLL + i
+                if a:
+                    scores(u, j)
+                if b:
+                    powers(u - 1, j)
+                if e:
+                    context(u - 2, j)
 
         close_unit(u, a, b, e)
 
-    def o_slot(yy, f, lo, n):
+    group = CHUNKS // 2
+
+    def o_slot(yy, f, g, lo, n):
         hh = half + f * (1 - 2 * half)
-        return panel.at[:, pl.ds(lo, n), pl.ds(pl.multiple_of((CORES * yy + hh) * chunk, chunk), chunk)]
-
-    def send_o(a):
+        return panel.at[pl.ds(g * group, group), pl.ds(lo, n), pl.ds(pl.multiple_of((CORES * yy + hh) * chunk, chunk), chunk)]
+
+    def send_o(a, g):
         return pltpu.make_async_remote_copy(
-            src_ref=obuf.at[:, pl.ds(a * Q_TILE, Q_TILE), :], dst_ref=o_slot(y, 0, a * Q_TILE, Q_TILE),
-            send_sem=t_send.at[a], recv_sem=t_recv.at[a], device_id=far, device_id_type=MESH)
-
-    def y_copy(f, a, way):
-        piece = o_slot(y, f, a * Q_TILE, Q_TILE)
-        return pltpu.make_async_remote_copy(src_ref=piece, dst_ref=piece, send_sem=y_send.at[f, a, way], recv_sem=y_recv.at[f, a, way], device_id=(up, down)[way], device_id_type=MESH)
-
-    def y_pass(f, a, way):
-        piece = o_slot((before, after)[way], f, a * Q_TILE + way * eighth, eighth)
-        return pltpu.make_async_remote_copy(src_ref=piece, dst_ref=piece, send_sem=y_send.at[f, a, 2 + way], recv_sem=y_recv.at[f, a, 2 + way], device_id=(up, down)[way], device_id_type=MESH)
+            src_ref=obuf.at[pl.ds(g * group, group), pl.ds(a * Q_TILE, Q_TILE), :], dst_ref=o_slot(y, 0, g, a * Q_TILE, Q_TILE),
+            send_sem=t_send.at[a, g], recv_sem=t_recv.at[a, g], device_id=far, device_id_type=MESH)
+
+    def y_copy(f, a, g, way):
+        piece = o_slot(y, f, g, a * Q_TILE, Q_TILE)
+        return pltpu.make_async_remote_copy(src_ref=piece, dst_ref=piece, send_sem=y_send.at[f, a, g, way], recv_sem=y_recv.at[f, a, g, way], device_id=(up, down)[way], device_id_type=MESH)
+
+    def y_pass(f, a, g, way):
+        piece = o_slot((before, after)[way], f, g, a * Q_TILE + way * eighth, eighth)
+        return pltpu.make_async_remote_copy(src_ref=piece, dst_ref=piece, send_sem=y_send.at[f, a, g, 2 + way], recv_sem=y_recv.at[f, a, g, 2 + way], device_id=(up, down)[way], device_id_type=MESH)
 
     def w_copy(kind, k):
         if kind == 0:
@@ -427,38 +434,41 @@
         (corner[k] if k < 2 else w_copy(0, k)).wait_recv()
         w_copy(3, k).start()
 
-    def y_start(f, a):
+    def y_start(f, a, g):
         for way in BOTH:
-            y_copy(f, a, way).start()
-
-    def y_relay(f, a):
+            y_copy(f, a, g, way).start()
+
+    def y_relay(f, a, g):
         for way in BOTH:
-            y_copy(f, a, way).wait_recv()
-            y_pass(f, a, way).start()
-
-    def o_in(a):
-        send_o(a).wait_recv()
-        y_start(1, a)
-
-    events = {
-        heads + 3: [lambda: y_start(0, 0), lambda: near_in(2), lambda: far_in(2)],
-        2 * heads + 3: [lambda: y_start(0, 1), lambda: y_relay(0, 0)],
-        2 * heads + 6: [lambda: near_in(3), lambda: far_in(3)],
-        3 * heads + 1: [lambda: y_relay(0, 1)],
-        3 * heads + 3: [lambda: send_o(0).start()],
-        4 * heads - 1: [lambda: corner_in(2)],
-    }
+            y_copy(f, a, g, way).wait_recv()
+            y_pass(f, a, g, way).start()
+
+    def o_in(a, g):
+        send_o(a, g).wait_recv()
+        y_start(1, a, g)
+
+    def o_out(a, g):
+        send_o(a, g).start()
+
+    events = (
+        (7, o_out, 0, 0), (11, o_out, 0, 1), (12, near_in, 2), (12, far_in, 2),
+        (15, o_out, 1, 0), (19, o_out, 1, 1), (19, o_in, 0, 0), (20, near_in, 3), (20, far_in, 3), (21, o_in, 0, 1),
+        (22, y_relay, 1, 0, 0), (23, y_start, 0, 0, 0), (24, y_relay, 1, 0, 1), (25, near_in, 1),
+        (26, y_relay, 0, 0, 0), (27, y_start, 0, 0, 1), (29, corner_in, 2), (30, y_relay, 0, 0, 1),
+        (30, o_in, 1, 0), (31, y_start, 0, 1, 0),
+    )
 
     unit(0, YES, NO, NO)
     unit(1, YES, YES, NO)
 
     @pl.loop(2, units)
     def _(u):
-        for at, steps in events.items():
+        for at in sorted({event[0] for event in events}):
             @pl.when(u == at)
-            def _(steps=steps):
-                for step in steps:
-                    step()
+            def _(at=at):
+                for when, step, *which in events:
+                    if when == at:
+                        step(*which)
         unit(u, YES, YES, YES)
 
     unit(units, NO, YES, YES)
@@ -480,40 +490,45 @@
             else:
                 out_ref[pl.ds(a * Q_TILE, Q_TILE), cols] = dot.astype(jnp.bfloat16)
 
-    o_in(0)
-    send_o(1).start()
+    def shares_in(k, kinds):
+        for kind in kinds:
+            w_copy(kind, k).wait_recv()
+
+    def rows_in(a, g):
+        for f in BOTH:
+            for way in BOTH:
+                y_pass(f, a, g, way).wait_recv()
+
+    passed = (1, 2, 3)
+    o_in(1, 1)
+    y_start(0, 1, 1)
+    y_relay(1, 1, 0)
+    y_relay(0, 1, 0)
     corner_in(0)
-    near_in(1)
-    y_relay(1, 0)
-    o_in(1)
-    for f in BOTH:
-        for way in BOTH:
-            y_pass(f, 0, way).wait_recv()
     for copy in placed:
         copy.wait()
     for copy in shared:
         copy.wait_recv()
-    for kind in (1, 2, 3):
-        w_copy(kind, 2).wait_recv()
+    rows_in(0, 0)
+    rows_in(0, 1)
+    shares_in(2, passed)
     multiply(0, 2, YES, NO)
+    y_relay(1, 1, 1)
+    y_relay(0, 1, 1)
+    shares_in(0, passed[2:])
+    multiply(0, 0, NO, NO)
+    rows_in(1, 0)
+    multiply(1, 0, YES, NO)
+    rows_in(1, 1)
+    multiply(1, 2, NO, NO)
     corner_in(3)
-    y_relay(1, 1)
-    w_copy(3, 0).wait_recv()
-    multiply(0, 0, NO, NO)
-    for kind in (1, 2, 3):
-        w_copy(kind, 3).wait_recv()
-    multiply(0, 3, NO, NO)
-    for f in BOTH:
-        for way in BOTH:
-            y_pass(f, 1, way).wait_recv()
-    multiply(1, 2, YES, NO)
     corner_in(1)
-    multiply(1, 0, NO, NO)
-    multiply(1, 3, NO, NO)
-    w_copy(1, 1).wait_recv()
-    w_copy(3, 1).wait_recv()
-    multiply(0, 1, NO, YES)
-    multiply(1, 1, NO, YES)
+    shares_in(3, passed)
+    for a in BOTH:
+        multiply(a, 3, NO, NO)
+    shares_in(1, passed[::2])
+    for a in BOTH:
+        multiply(a, 1, NO, YES)
     for copy in started:
         copy.wait_send()
     for k in (2, 3):
@@ -523,11 +538,12 @@
     for kind, k in ((3, 0), (1, 1), (3, 1)):
         w_copy(kind, k).wait_send()
     for a in BOTH:
-        send_o(a).wait_send()
-        for f in BOTH:
-            for way in BOTH:
-                y_copy(f, a, way).wait_send()
-                y_pass(f, a, way).wait_send()
+        for g in BOTH:
+            send_o(a, g).wait_send()
+            for f in BOTH:
+                for way in BOTH:
+                    y_copy(f, a, g, way).wait_send()
+                    y_pass(f, a, g, way).wait_send()
 
 
 def attend_project(q, kv, segs, got, w_out, n_x, n_y):
@@ -553,8 +569,8 @@
             pltpu.VMEM((3, Q_TILE, 128), jnp.float32),
             pltpu.VMEM((Q_TILE, HEAD_DIM), jnp.float32),
             dma((CHUNKS, 2)), dma((CHUNKS, 2)), dma((CHUNKS, 2)), dma((CHUNKS, 2)),
-            dma((CHUNKS, 4)), dma((CHUNKS, 4)), dma((2,)), dma((2,)),
-            dma((2, 2, 4)), dma((2, 2, 4)), dma((CHUNKS + 3,)),
+            dma((CHUNKS, 4)), dma((CHUNKS, 4)), dma((2, 2)), dma((2, 2)),
+            dma((2, 2, 2, 4)), dma((2, 2, 2, 4)), dma((CHUNKS + 3,)),
         ],
         compiler_params=pltpu.CompilerParams(collective_id=1, has_side_effects=YES, vmem_limit_bytes=63 * 1024 * 1024),
         cost_estimate=pl.CostEstimate(flops=8 * rows * ctx * keys, bytes_accessed=4 * depth * width, transcendentals=0),

time: 373 us -> 346 us (0.928)
  Pallas kernels: 369 us -> 342 us
    pallas_call x1, Pallas kernels: 208 us -> 181 us  [attend_project(): pl.pallas_call(functools.partial(attend_kernel, n_x, n_y), out_shape=jax....]
where the time goes in v1:
time: 346 us
  Pallas kernels  342 us (99%)
    pallas_call x1, Pallas kernels, attend_project(): pl.pallas_call(functools.partial(attend_kernel, n_x, n_y), out_shape=jax....  181 us
    pallas_call x1, Pallas kernels, project_qkv(): pl.pallas_call(functools.partial(qkv_kernel, n_x, n_y), out_shape=(jax.Sh...  161 us

profile of v1, /device:TPU:97, one launch (start us, length us, event | category | flops | bytes accessed | tf_op | source)
XLA Modules:
  0.0 345.6 jit_solution(16142152750605008612)
XLA Ops:
  0.0 161.2 %project_qkv.1 = (bf16[1024,1024]{1,0:T(8,128)(2,1)}, bf16[4096,256]{1,0:T(8,128)(2,1)}, s32[8,4,128]{2,1,0:T(4,128)}, bf16[3,256,2048]{2,1,0:T(8,128)(2,1)}) custom-call(bf16[512,2048]{1,0:T(8,128)(2,1)} %tok_ref.1, bf16[1024,2560]{1,0:T(8,128)(2,1)} %w_ref.2, bf16[1024,2048]{1,0:T(8,128)(2,1)} %w_ref.3, s32[4,128]{1,0:T(4,128)} %bitcast.1), custom_call_target="tpu_custom_call" | custom-call | flops 21474836480 | bytes 5242880 | tf_op jit(solution)/shard_map/project_qkv/pallas_call | solution.py:221
  161.2 181.2 %attend_project.1 = bf16[512,2048]{1,0:T(8,128)(2,1)} custom-call(bf16[1024,1024]{1,0:T(8,128)(2,1)} %get-tuple-element.9.q_ref, bf16[4096,256]{1,0:T(8,128)(2,1)} %get-tuple-element.10.kv_ref, s32[8,4,128]{2,1,0:T(4,128)} %get-tuple-element.11.segs_ref, bf16[3,256,2048]{2,1,0:T(8,128)(2,1)} %get-tuple-element.12.got_ref, bf16[1024,2048]{1,0:T(8,128)(2,1)} %w_ref.3), custom_call_target="tpu_custom_call" | custom-call | flops 17179869184 | bytes 8388608 | tf_op jit(solution)/shard_map/attend_project/pallas_call | solution.py:557
  342.4 3.2 copy.6

commit v2 on v1

--- a/solution.py
+++ b/solution.py
@@ -24,7 +24,7 @@
     return x + 1 - 2 * (x % 2)
 
 
-def qkv_kernel(n_x, n_y, tok_ref, w_ref, wo_ref, seg_ref, q_ref, kv_ref, segs_ref, got_ref, xg, wg, acc, w_send, w_recv, d_send, d_recv, t_send, t_recv, y_send, y_recv, k_send, k_recv, l_sem, s_send, s_recv, o_send, o_recv):
+def qkv_kernel(n_x, n_y, tok_ref, w_ref, wo_ref, seg_ref, q_ref, kv_ref, segs_ref, got_ref, xg, wg, acc, w_send, w_recv, d_send, d_recv, t_send, t_recv, y_send, y_recv, k_send, k_recv, s_send, s_recv, o_send, o_recv, l_sem):
     r, y = lax.axis_index("row"), lax.axis_index("col")
     x, c = r // CORES, r % CORES
     xn, xf = near_x(x), n_x - 1 - x
@@ -232,9 +232,8 @@
             pltpu.VMEM((2, n_y, rows, width), jnp.bfloat16),
             pltpu.VMEM((n_x, CORES * depth, part), jnp.bfloat16),
             pltpu.VMEM((rows, part), jnp.float32),
-            dma((3, 2)), dma((3, 2)), dma((4, 2)), dma((4, 2)), dma((2,)), dma((2,)),
-            dma((2, 2, 4)), dma((2, 2, 4)), dma((6,)), dma((6,)), dma((3,)),
-            dma((n_row - 1,)), dma((n_row - 1,)), dma((3,)), dma((3,)),
+            *[dma(shape) for shape in ((3, 2), (4, 2), (2,), (2, 2, 4), (6,), (n_row - 1,), (3,)) for _ in BOTH],
+            dma((3,)),
         ],
         compiler_params=pltpu.CompilerParams(collective_id=0, has_side_effects=YES, vmem_limit_bytes=60 * 1024 * 1024),
         cost_estimate=pl.CostEstimate(flops=4 * rows * n_y * width * part, bytes_accessed=2 * depth * cols, transcendentals=0),
@@ -242,7 +241,7 @@
     )(tokens, w_qkv, w_out, segs)
 
 
-def attend_kernel(n_x, n_y, q_ref, kv_ref, segs_ref, got_ref, w_ref, out_ref, wo, panel, obuf, sbuf, segq, mbuf, lbuf, abuf, n_send, n_recv, f_send, f_recv, d_send, d_recv, t_send, t_recv, y_send, y_recv, l_sem):
+def attend_kernel(n_x, n_y, q_ref, kv_ref, segs_ref, got_ref, w_ref, out_ref, wo, panel, obuf, buf_a, buf_b, buf_c, segq, mbuf, lbuf, abuf, n_send, n_recv, f_send, f_recv, d_send, d_recv, t_send, t_recv, y_send, y_recv, l_sem):
     r, y = lax.axis_index("row"), lax.axis_index("col")
     x, c = r // CORES, r % CORES
     xn, xf = near_x(x), n_x - 1 - x
@@ -285,17 +284,23 @@
         slot = w_slot(k, (x, xn, xf, xnf)[origin])
         return send(slot if src is None else src, slot, d_send.at[k, origin], d_recv.at[k, origin], core)
 
-    def to_near(k, src, chip):
-        return send(src, w_slot(k, chip), n_send.at[k, 0], n_recv.at[k, 0], near)
-
-    def to_far(k, src, chip):
-        return send(src, w_slot(k, chip), f_send.at[k, 0], f_recv.at[k, 0], far)
-
-    direct = {2: to_near(2, w_mine(2), x), 3: to_near(3, w_mine(3), x)}
-    straight = {2: to_far(2, w_mine(2), x), 3: to_far(3, w_mine(3), x)}
-    direct[1] = to_near(1, w_mine(1), x)
-    corner = {0: send(got_ref.at[1], w_slot(0, xf), n_send.at[0, 1], n_recv.at[0, 1], near)}
-    corner[1] = send(got_ref.at[2], w_slot(1, xf), n_send.at[1, 1], n_recv.at[1, 1], near)
+    def remote(src, dst, s_sem, r_sem, peer):
+        return pltpu.make_async_remote_copy(src_ref=src, dst_ref=dst, send_sem=s_sem, recv_sem=r_sem, device_id=peer, device_id_type=MESH)
+
+    def to_near(k):
+        return remote(w_mine(k), w_slot(k, x), n_send.at[k, 0], n_recv.at[k, 0], near)
+
+    def to_far(k):
+        return remote(w_mine(k), w_slot(k, x), f_send.at[k, 0], f_recv.at[k, 0], far)
+
+    def corner(k):
+        return remote(got_ref.at[1 + k], w_slot(k, xf), n_send.at[k, 1], n_recv.at[k, 1], near)
+
+    def begin(copy, k):
+        copy(k).start()
+
+    begin(to_near, 2)
+    begin(to_far, 2)
     places = [(w_mine(k), w_slot(k, x)) for k in range(CHUNKS)]
     places += [(got_ref.at[0], w_slot(0, xn)), (got_ref.at[1], w_slot(0, xf)), (got_ref.at[2], w_slot(1, xf))]
     placed = [pltpu.make_async_copy(src, dst, l_sem.at[i]) for i, (src, dst) in enumerate(places)]
@@ -317,9 +322,11 @@
 
     blocks = keys // rows
     lanes = rows // 128
-
-    def scores(u, j):
-        b, tile, h = u % 3, (u // heads + tiles // 2) % tiles, u % heads
+    bufs = (buf_a, buf_b, buf_c)
+    n_buf = len(bufs)
+
+    def scores(b, u, j):
+        tile, h = (u // heads + tiles // 2) % tiles, u % heads
         q = q_ref[pl.ds(pl.multiple_of(tile * Q_TILE, Q_TILE), Q_TILE), pl.ds(pl.multiple_of(h * HEAD_DIM, HEAD_DIM), HEAD_DIM)]
         k = kv_ref[pl.ds(pl.multiple_of(j * rows, rows), rows), pl.ds(0, HEAD_DIM)]
         s = lax.dot_general(q, k, (((1,), (1,)), ((), ())), preferred_element_type=jnp.float32)
@@ -328,40 +335,38 @@
         top = mbuf[b]
         for i in range(lanes):
             part = jnp.where(own == seg[i:i + 1, :], s[:, i * 128:(i + 1) * 128], lowest)
-            sbuf[b, j * lanes + i] = part
+            bufs[b][j * lanes + i] = part
             top = jnp.maximum(top, part)
         mbuf[b] = top
 
-    def powers(u, j):
-        b = u % 3
+    def powers(b, j):
         top = mbuf[b]
         total = lbuf[b]
         for i in range(lanes):
-            e = jnp.exp2((sbuf[b, j * lanes + i] - top) * coef)
-            sbuf[b, j * lanes + i] = e
+            e = jnp.exp2((bufs[b][j * lanes + i] - top) * coef)
+            bufs[b][j * lanes + i] = e
             total = total + e
         lbuf[b] = total
 
-    def context(u, j):
-        b = u % 3
+    def context(b, j):
         inv = lbuf[b]
-        p = jnp.concatenate([(sbuf[b, j * lanes + i] * inv).astype(jnp.bfloat16) for i in range(lanes)], axis=1)
+        p = jnp.concatenate([(bufs[b][j * lanes + i] * inv).astype(jnp.bfloat16) for i in range(lanes)], axis=1)
         v = kv_ref[pl.ds(pl.multiple_of(j * rows, rows), rows), pl.ds(HEAD_DIM, HEAD_DIM)]
         abuf[...] += jnp.dot(p, v, preferred_element_type=jnp.float32)
 
-    def open_unit(u, a, b, e):
+    def open_unit(s, a, b, e):
         if a:
-            mbuf[u % 3] = jnp.full(mbuf.shape[1:], lowest, jnp.float32)
+            mbuf[s] = jnp.full(mbuf.shape[1:], lowest, jnp.float32)
         if b:
-            lbuf[(u - 1) % 3] = jnp.zeros(lbuf.shape[1:], jnp.float32)
+            lbuf[(s - 1) % n_buf] = jnp.zeros(lbuf.shape[1:], jnp.float32)
         if e:
             abuf[...] = jnp.zeros(abuf.shape, jnp.float32)
 
-    def close_unit(u, a, b, e):
+    def close_unit(s, u, a, b, e):
         if a:
-            mbuf[u % 3] = jnp.broadcast_to(jnp.max(mbuf[u % 3], axis=1, keepdims=YES), mbuf.shape[1:])
+            mbuf[s] = jnp.broadcast_to(jnp.max(mbuf[s], axis=1, keepdims=YES), mbuf.shape[1:])
         if b:
-            lbuf[(u - 1) % 3] = 1.0 / jnp.broadcast_to(jnp.sum(lbuf[(u - 1) % 3], axis=1, keepdims=YES), lbuf.shape[1:])
+            lbuf[(s - 1) % n_buf] = 1.0 / jnp.broadcast_to(jnp.sum(lbuf[(s - 1) % n_buf], axis=1, keepdims=YES), lbuf.shape[1:])
         if e:
             tile, h = (u - 2) // heads, (u - 2) % heads
             out = abuf[...].astype(jnp.bfloat16)
@@ -379,21 +384,21 @@
             def _():
                 obuf[h // per, at, pl.ds(lo, HEAD_DIM)] = out
 
-    def unit(u, a, b, e):
-        open_unit(u, a, b, e)
+    def unit(s, u, a, b, e):
+        open_unit(s, a, b, e)
 
         @pl.loop(0, blocks // UNROLL)
         def _(jj):
             for i in range(UNROLL):
                 j = jj * UNROLL + i
                 if a:
-                    scores(u, j)
+                    scores(s, u, j)
                 if b:
-                    powers(u - 1, j)
+                    powers((s - 1) % n_buf, j)
                 if e:
-                    context(u - 2, j)
-
-        close_unit(u, a, b, e)
+                    context((s - 2) % n_buf, j)
+
+        close_unit(s, u, a, b, e)
 
     group = CHUNKS // 2
 
@@ -416,22 +421,22 @@
 
     def w_copy(kind, k):
         if kind == 0:
-            return pltpu.make_async_remote_copy(src_ref=w_slot(k, xn), dst_ref=w_slot(k, xn), send_sem=f_send.at[k, 1], recv_sem=f_recv.at[k, 1], device_id=far, device_id_type=MESH)
+            return remote(w_slot(k, xn), w_slot(k, xn), f_send.at[k, 1], f_recv.at[k, 1], far)
         slot = w_slot(k, (x, xn, xf, xnf)[kind])
         return pltpu.make_async_remote_copy(src_ref=slot, dst_ref=slot, send_sem=d_send.at[k, kind], recv_sem=d_recv.at[k, kind], device_id=core, device_id_type=MESH)
 
     def near_in(k):
-        direct[k].wait_recv()
+        to_near(k).wait_recv()
         if k >= 2:
             w_copy(0, k).start()
         w_copy(1, k).start()
 
     def far_in(k):
-        straight[k].wait_recv()
+        to_far(k).wait_recv()
         w_copy(2, k).start()
 
     def corner_in(k):
-        (corner[k] if k < 2 else w_copy(0, k)).wait_recv()
+        (corner(k) if k < 2 else w_copy(0, k)).wait_recv()
         w_copy(3, k).start()
 
     def y_start(f, a, g):
@@ -451,28 +456,31 @@
         send_o(a, g).start()
 
     events = (
+        (5, begin, to_near, 3), (6, begin, to_far, 3), (13, begin, to_near, 1), (22, begin, corner, 0), (29, begin, corner, 1),
         (7, o_out, 0, 0), (11, o_out, 0, 1), (12, near_in, 2), (12, far_in, 2),
         (15, o_out, 1, 0), (19, o_out, 1, 1), (19, o_in, 0, 0), (20, near_in, 3), (20, far_in, 3), (21, o_in, 0, 1),
-        (22, y_relay, 1, 0, 0), (23, y_start, 0, 0, 0), (24, y_relay, 1, 0, 1), (25, near_in, 1),
+        (22, y_relay, 1, 0, 0), (23, y_start, 0, 0, 0), (24, y_relay, 1, 0, 1), (28, near_in, 1),
         (26, y_relay, 0, 0, 0), (27, y_start, 0, 0, 1), (29, corner_in, 2), (30, y_relay, 0, 0, 1),
         (30, o_in, 1, 0), (31, y_start, 0, 1, 0),
     )
 
-    unit(0, YES, NO, NO)
-    unit(1, YES, YES, NO)
-
-    @pl.loop(2, units)
-    def _(u):
-        for at in sorted({event[0] for event in events}):
-            @pl.when(u == at)
-            def _(at=at):
-                for when, step, *which in events:
-                    if when == at:
-                        step(*which)
-        unit(u, YES, YES, YES)
-
-    unit(units, NO, YES, YES)
-    unit(units + 1, NO, NO, YES)
+    unit(0, 0, YES, NO, NO)
+    unit(1, 1, YES, YES, NO)
+
+    @pl.loop(0, (units - 2) // n_buf)
+    def _(i):
+        for s in range(n_buf):
+            for at in sorted({event[0] for event in events}):
+                if (at - 2) % n_buf == s:
+                    @pl.when(i == (at - 2) // n_buf)
+                    def _(at=at):
+                        for when, step, *which in events:
+                            if when == at:
+                                step(*which)
+            unit((s + 2) % n_buf, 2 + i * n_buf + s, YES, YES, YES)
+
+    unit(units % n_buf, units, NO, YES, YES)
+    unit((units + 1) % n_buf, units + 1, NO, NO, YES)
 
     def multiply(a, k, first, last):
         tile = 2 * HEAD_DIM
@@ -483,10 +491,10 @@
             dot = jnp.dot(panel[k, pl.ds(a * Q_TILE, Q_TILE), :], wo[k, :, cols], preferred_element_type=jnp.float32)
             per = tile // 128
             if not first:
-                dot = dot + jnp.concatenate([sbuf[a, n * per + i] for i in range(per)], axis=1)
+                dot = dot + jnp.concatenate([bufs[a][n * per + i] for i in range(per)], axis=1)
             if not last:
                 for i in range(per):
-                    sbuf[a, n * per + i] = dot[:, i * 128:(i + 1) * 128]
+                    bufs[a][n * per + i] = dot[:, i * 128:(i + 1) * 128]
             else:
                 out_ref[pl.ds(a * Q_TILE, Q_TILE), cols] = dot.astype(jnp.bfloat16)
 
@@ -531,7 +539,12 @@
         multiply(a, 1, NO, YES)
     for copy in started:
         copy.wait_send()
+    to_near(1).wait_send()
+    for k in BOTH:
+        corner(k).wait_send()
     for k in (2, 3):
+        to_near(k).wait_send()
+        to_far(k).wait_send()
         w_copy(0, k).wait_send()
         for kind in (1, 2, 3):
             w_copy(kind, k).wait_send()
@@ -563,14 +576,15 @@
             pltpu.VMEM((CHUNKS, n_row * chunk, width), jnp.bfloat16),
             pltpu.VMEM((CHUNKS, rows, n_row * chunk), jnp.bfloat16),
             pltpu.VMEM((CHUNKS, rows, chunk), jnp.bfloat16),
-            pltpu.VMEM((3, keys // 128, Q_TILE, 128), jnp.float32),
+            pltpu.VMEM((keys // 128, Q_TILE, 128), jnp.float32),
+            pltpu.VMEM((keys // 128, Q_TILE, 128), jnp.float32),
+            pltpu.VMEM((keys // 128, Q_TILE, 128), jnp.float32),
             pltpu.VMEM((2 * rows, 128), jnp.float32),
             pltpu.VMEM((3, Q_TILE, 128), jnp.float32),
             pltpu.VMEM((3, Q_TILE, 128), jnp.float32),
             pltpu.VMEM((Q_TILE, HEAD_DIM), jnp.float32),
-            dma((CHUNKS, 2)), dma((CHUNKS, 2)), dma((CHUNKS, 2)), dma((CHUNKS, 2)),
-            dma((CHUNKS, 4)), dma((CHUNKS, 4)), dma((2, 2)), dma((2, 2)),
-            dma((2, 2, 2, 4)), dma((2, 2, 2, 4)), dma((CHUNKS + 3,)),
+            *[dma(shape) for shape in ((CHUNKS, 2), (CHUNKS, 2), (CHUNKS, 4), (2, 2), (2, 2, 2, 4)) for _ in BOTH],
+            dma((CHUNKS + 3,)),
         ],
         compiler_params=pltpu.CompilerParams(collective_id=1, has_side_effects=YES, vmem_limit_bytes=63 * 1024 * 1024),
         cost_estimate=pl.CostEstimate(flops=8 * rows * ctx * keys, bytes_accessed=4 * depth * width, transcendentals=0),

time: 346 us -> 319 us (0.922)
  Pallas kernels: 342 us -> 316 us
    pallas_call x1, Pallas kernels: 181 us -> 154 us  [attend_project(): pl.pallas_call(functools.partial(attend_kernel, n_x, n_y), out_shape=jax....]
where the time goes in v2:
time: 319 us
  Pallas kernels  316 us (99%)
    pallas_call x1, Pallas kernels, project_qkv(): pl.pallas_call(functools.partial(qkv_kernel, n_x, n_y), out_shape=(jax.Sh...  161 us
    pallas_call x1, Pallas kernels, attend_project(): pl.pallas_call(functools.partial(attend_kernel, n_x, n_y), out_shape=jax....  154 us

profile of v2, /device:TPU:97, one launch (start us, length us, event | category | flops | bytes accessed | tf_op | source)
XLA Modules:
  0.0 318.8 jit_solution(17212953221184438331)
XLA Ops:
  0.0 161.2 %project_qkv.1 = (bf16[1024,1024]{1,0:T(8,128)(2,1)}, bf16[4096,256]{1,0:T(8,128)(2,1)}, s32[8,4,128]{2,1,0:T(4,128)}, bf16[3,256,2048]{2,1,0:T(8,128)(2,1)}) custom-call(bf16[512,2048]{1,0:T(8,128)(2,1)} %tok_ref.1, bf16[1024,2560]{1,0:T(8,128)(2,1)} %w_ref.2, bf16[1024,2048]{1,0:T(8,128)(2,1)} %w_ref.3, s32[4,128]{1,0:T(4,128)} %bitcast.1), custom_call_target="tpu_custom_call" | custom-call | flops 21474836480 | bytes 5242880 | tf_op jit(solution)/shard_map/project_qkv/pallas_call | solution.py:221
  161.2 154.5 %attend_project.1 = bf16[512,2048]{1,0:T(8,128)(2,1)} custom-call(bf16[1024,1024]{1,0:T(8,128)(2,1)} %get-tuple-element.9.q_ref, bf16[4096,256]{1,0:T(8,128)(2,1)} %get-tuple-element.10.kv_ref, s32[8,4,128]{2,1,0:T(4,128)} %get-tuple-element.11.segs_ref, bf16[3,256,2048]{2,1,0:T(8,128)(2,1)} %get-tuple-element.12.got_ref, bf16[1024,2048]{1,0:T(8,128)(2,1)} %w_ref.3), custom_call_target="tpu_custom_call" | custom-call | flops 17179869184 | bytes 8388608 | tf_op jit(solution)/shard_map/attend_project/pallas_call | solution.py:570
  315.7 3.2 copy.6

commit v3 on v2

--- a/solution.py
+++ b/solution.py
@@ -88,15 +88,14 @@
         return send(piece, piece, y_send.at[b, a, 2 + way], y_recv.at[b, a, 2 + way], (up, down)[way])
 
     segs = [send(seg_ref, segs_ref.at[r], s_send.at[d], s_recv.at[d], peer) for d, peer in enumerate(row_peers)]
+    chunk = depth // CHUNKS
+
+    def give_wo(i):
+        return send(wo_ref.at[pl.ds(i * chunk, chunk), :], got_ref.at[1 + i], o_send.at[1 + i], o_recv.at[1 + i], far)
+
     w_far = [send_w(1, 0)]
-    y_own = [[send_y(0, a, way) for way in BOTH] for a in BOTH]
     w_near = [send_w(0, 0)]
-    tok = [send_t(0)]
-    w_near.append(send_w(0, 1))
-    w_far.append(send_w(1, 1))
-    tok.append(send_t(1))
-    chunk = depth // CHUNKS
-    wo_got = [send(wo_ref.at[pl.ds(i * chunk, chunk), :], got_ref.at[1 + i], o_send.at[1 + i], o_recv.at[1 + i], far) for i in BOTH]
+    y_own = [[send_y(0, 0, way) for way in BOTH]]
     locals_ = [
         pltpu.make_async_copy(seg_ref, segs_ref.at[r], l_sem.at[2]),
         pltpu.make_async_copy(tok_ref, xg.at[0, y], l_sem.at[0]),
@@ -145,14 +144,18 @@
         return got
 
     y_far = [relay(0, 0)]
+    y_own.append([send_y(0, 1, way) for way in BOTH])
+    tok = [send_t(0)]
+    w_near.append(send_w(0, 1))
+    w_near[0].wait_recv()
+    d_near = [share(xn, 0, 1)]
     w_far[0].wait_recv()
     w_nf = [send_w(2, 0)]
     d_far = [share(xf, 0, 2)]
-    w_near[0].wait_recv()
-    d_near = [share(xn, 0, 1)]
+    tok[0].wait_recv()
+    w_far.append(send_w(1, 1))
+    y_par = [[send_y(1, 0, way) for way in BOTH]]
     y_far.append(relay(0, 1))
-    tok[0].wait_recv()
-    y_par = [[send_y(1, 0, way) for way in BOTH]]
     w_near[1].wait_recv()
     d_near.append(share(xn, 1, 1))
     for pair in y_far:
@@ -163,22 +166,25 @@
     for copy in d_own:
         copy.wait_recv()
     multiply(0, 0, rows, x, YES, NO)
+    tok.append(send_t(1))
     for copy in d_near:
         copy.wait_recv()
+    multiply(0, 0, rows, xn, NO, NO)
     w_far[1].wait_recv()
     w_nf.append(send_w(2, 1))
-    wo_got.append(send(wo_ref.at[pl.ds(0, chunk), :], got_ref.at[0], o_send.at[0], o_recv.at[0], near))
     d_far.append(share(xf, 1, 2))
-    multiply(0, 0, rows, xn, NO, NO)
+    y_pfar = [relay(1, 0)]
     w_nf[0].wait_recv()
     d_nf = [share(xnf, 0, 3)]
-    y_pfar = [relay(1, 0)]
+    for copy in d_far:
+        copy.wait_recv()
+    multiply(0, 0, rows, xf, NO, NO)
     tok[1].wait_recv()
     y_par.append([send_y(1, 1, way) for way in BOTH])
-    for copy in d_far:
-        copy.wait_recv()
-    multiply(0, 0, rows, xf, NO, NO)
+    wo_got = [give_wo(0)]
     w_nf[1].wait_recv()
+    wo_got.append(send(wo_ref.at[pl.ds(0, chunk), :], got_ref.at[0], o_send.at[0], o_recv.at[0], near))
+    wo_got.append(give_wo(1))
     d_nf.append(share(xnf, 1, 3))
     for copy in d_nf:
         copy.wait_recv()
@@ -456,12 +462,11 @@
         send_o(a, g).start()
 
     events = (
-        (5, begin, to_near, 3), (6, begin, to_far, 3), (13, begin, to_near, 1), (22, begin, corner, 0), (29, begin, corner, 1),
-        (7, o_out, 0, 0), (11, o_out, 0, 1), (12, near_in, 2), (12, far_in, 2),
-        (15, o_out, 1, 0), (19, o_out, 1, 1), (19, o_in, 0, 0), (20, near_in, 3), (20, far_in, 3), (21, o_in, 0, 1),
-        (22, y_relay, 1, 0, 0), (23, y_start, 0, 0, 0), (24, y_relay, 1, 0, 1), (28, near_in, 1),
-        (26, y_relay, 0, 0, 0), (27, y_start, 0, 0, 1), (29, corner_in, 2), (30, y_relay, 0, 0, 1),
-        (30, o_in, 1, 0), (31, y_start, 0, 1, 0),
+        (5, begin, to_near, 3), (7, o_out, 0, 0), (8, begin, to_far, 3), (11, o_out, 0, 1), (13, begin, to_near, 1),
+        (15, o_out, 1, 0), (19, o_out, 1, 1), (19, o_in, 0, 0), (20, near_in, 2), (20, far_in, 2), (21, o_in, 0, 1),
+        (22, begin, corner, 0), (23, y_relay, 1, 0, 0), (23, y_start, 0, 0, 0), (25, y_relay, 1, 0, 1),
+        (27, y_relay, 0, 0, 0), (27, y_start, 0, 0, 1), (28, near_in, 3), (28, far_in, 3), (28, near_in, 1),
+        (29, begin, corner, 1), (29, o_in, 1, 0), (31, y_relay, 0, 0, 1), (31, y_start, 0, 1, 0),
     )
 
     unit(0, 0, YES, NO, NO)
@@ -512,6 +517,7 @@
     y_start(0, 1, 1)
     y_relay(1, 1, 0)
     y_relay(0, 1, 0)
+    corner_in(2)
     corner_in(0)
     for copy in placed:
         copy.wait()
@@ -530,10 +536,10 @@
     rows_in(1, 1)
     multiply(1, 2, NO, NO)
     corner_in(3)
+    shares_in(3, passed)
+    multiply(0, 3, NO, NO)
     corner_in(1)
-    shares_in(3, passed)
-    for a in BOTH:
-        multiply(a, 3, NO, NO)
+    multiply(1, 3, NO, NO)
     shares_in(1, passed[::2])
     for a in BOTH:
         multiply(a, 1, NO, YES)

time: 319 us -> 332 us (1.041)
  Pallas kernels: 316 us -> 329 us
    pallas_call x1, Pallas kernels: 161 us -> 177 us  [project_qkv(): pl.pallas_call(functools.partial(qkv_kernel, n_x, n_y), out_shape=(jax.Sh...]
where the time goes in v3:
time: 332 us
  Pallas kernels  329 us (99%)
    pallas_call x1, Pallas kernels, project_qkv(): pl.pallas_call(functools.partial(qkv_kernel, n_x, n_y), out_shape=(jax.Sh...  177 us
    pallas_call x1, Pallas kernels, attend_project(): pl.pallas_call(functools.partial(attend_kernel, n_x, n_y), out_shape=jax....  152 us

profile of v3, /device:TPU:97, one launch (start us, length us, event | category | flops | bytes accessed | tf_op | source)
XLA Modules:
  0.0 331.8 jit_solution(7520886161971600767)
XLA Ops:
  0.0 177.1 %project_qkv.1 = (bf16[1024,1024]{1,0:T(8,128)(2,1)}, bf16[4096,256]{1,0:T(8,128)(2,1)}, s32[8,4,128]{2,1,0:T(4,128)}, bf16[3,256,2048]{2,1,0:T(8,128)(2,1)}) custom-call(bf16[512,2048]{1,0:T(8,128)(2,1)} %tok_ref.1, bf16[1024,2560]{1,0:T(8,128)(2,1)} %w_ref.2, bf16[1024,2048]{1,0:T(8,128)(2,1)} %w_ref.3, s32[4,128]{1,0:T(4,128)} %bitcast.1), custom_call_target="tpu_custom_call" | custom-call | flops 21474836480 | bytes 5242880 | tf_op jit(solution)/shard_map/project_qkv/pallas_call | solution.py:227
  177.1 151.6 %attend_project.1 = bf16[512,2048]{1,0:T(8,128)(2,1)} custom-call(bf16[1024,1024]{1,0:T(8,128)(2,1)} %get-tuple-element.9.q_ref, bf16[4096,256]{1,0:T(8,128)(2,1)} %get-tuple-element.10.kv_ref, s32[8,4,128]{2,1,0:T(4,128)} %get-tuple-element.11.segs_ref, bf16[3,256,2048]{2,1,0:T(8,128)(2,1)} %get-tuple-element.12.got_ref, bf16[1024,2048]{1,0:T(8,128)(2,1)} %w_ref.3), custom_call_target="tpu_custom_call" | custom-call | flops 17179869184 | bytes 8388608 | tf_op jit(solution)/shard_map/attend_project/pallas_call | solution.py:576
  328.7 3.2 copy.6

commit v4 on v2

--- a/solution.py
+++ b/solution.py
@@ -96,7 +96,6 @@
     w_far.append(send_w(1, 1))
     tok.append(send_t(1))
     chunk = depth // CHUNKS
-    wo_got = [send(wo_ref.at[pl.ds(i * chunk, chunk), :], got_ref.at[1 + i], o_send.at[1 + i], o_recv.at[1 + i], far) for i in BOTH]
     locals_ = [
         pltpu.make_async_copy(seg_ref, segs_ref.at[r], l_sem.at[2]),
         pltpu.make_async_copy(tok_ref, xg.at[0, y], l_sem.at[0]),
@@ -153,6 +152,7 @@
     y_far.append(relay(0, 1))
     tok[0].wait_recv()
     y_par = [[send_y(1, 0, way) for way in BOTH]]
+    wo_got = [send(wo_ref.at[pl.ds(i * chunk, chunk), :], got_ref.at[1 + i], o_send.at[1 + i], o_recv.at[1 + i], far) for i in BOTH]
     w_near[1].wait_recv()
     d_near.append(share(xn, 1, 1))
     for pair in y_far:
@@ -456,12 +456,11 @@
         send_o(a, g).start()
 
     events = (
-        (5, begin, to_near, 3), (6, begin, to_far, 3), (13, begin, to_near, 1), (22, begin, corner, 0), (29, begin, corner, 1),
-        (7, o_out, 0, 0), (11, o_out, 0, 1), (12, near_in, 2), (12, far_in, 2),
-        (15, o_out, 1, 0), (19, o_out, 1, 1), (19, o_in, 0, 0), (20, near_in, 3), (20, far_in, 3), (21, o_in, 0, 1),
-        (22, y_relay, 1, 0, 0), (23, y_start, 0, 0, 0), (24, y_relay, 1, 0, 1), (28, near_in, 1),
-        (26, y_relay, 0, 0, 0), (27, y_start, 0, 0, 1), (29, corner_in, 2), (30, y_relay, 0, 0, 1),
-        (30, o_in, 1, 0), (31, y_start, 0, 1, 0),
+        (3, begin, to_near, 3), (4, begin, to_far, 3), (7, o_out, 0, 0), (10, begin, to_near, 1), (11, o_out, 0, 1),
+        (15, o_out, 1, 0), (16, near_in, 2), (17, begin, corner, 0), (19, o_out, 1, 1), (19, o_in, 0, 0), (20, far_in, 2),
+        (21, o_in, 0, 1), (23, y_relay, 1, 0, 0), (23, y_start, 0, 0, 0), (24, begin, corner, 1), (25, near_in, 3),
+        (25, y_relay, 1, 0, 1), (27, y_relay, 0, 0, 0), (27, y_start, 0, 0, 1), (28, far_in, 3), (29, near_in, 1),
+        (29, o_in, 1, 0), (31, y_relay, 0, 0, 1), (31, y_start, 0, 1, 0),
     )
 
     unit(0, 0, YES, NO, NO)
@@ -512,6 +511,7 @@
     y_start(0, 1, 1)
     y_relay(1, 1, 0)
     y_relay(0, 1, 0)
+    corner_in(2)
     corner_in(0)
     for copy in placed:
         copy.wait()
@@ -530,10 +530,10 @@
     rows_in(1, 1)
     multiply(1, 2, NO, NO)
     corner_in(3)
+    shares_in(3, passed)
+    multiply(0, 3, NO, NO)
     corner_in(1)
-    shares_in(3, passed)
-    for a in BOTH:
-        multiply(a, 3, NO, NO)
+    multiply(1, 3, NO, NO)
     shares_in(1, passed[::2])
     for a in BOTH:
         multiply(a, 1, NO, YES)

time: 319 us -> 317 us (level)
  no operation moved by 1% of the time
where the time goes in v4:
time: 317 us
  Pallas kernels  314 us (99%)
    pallas_call x1, Pallas kernels, project_qkv(): pl.pallas_call(functools.partial(qkv_kernel, n_x, n_y), out_shape=(jax.Sh...  161 us
    pallas_call x1, Pallas kernels, attend_project(): pl.pallas_call(functools.partial(attend_kernel, n_x, n_y), out_shape=jax....  153 us

profile of v4, /device:TPU:97, one launch (start us, length us, event | category | flops | bytes accessed | tf_op | source)
XLA Modules:
  0.0 317.3 jit_solution(16024526856658596973)
XLA Ops:
  0.0 161.2 %project_qkv.1 = (bf16[1024,1024]{1,0:T(8,128)(2,1)}, bf16[4096,256]{1,0:T(8,128)(2,1)}, s32[8,4,128]{2,1,0:T(4,128)}, bf16[3,256,2048]{2,1,0:T(8,128)(2,1)}) custom-call(bf16[512,2048]{1,0:T(8,128)(2,1)} %tok_ref.1, bf16[1024,2560]{1,0:T(8,128)(2,1)} %w_ref.2, bf16[1024,2048]{1,0:T(8,128)(2,1)} %w_ref.3, s32[4,128]{1,0:T(4,128)} %bitcast.1), custom_call_target="tpu_custom_call" | custom-call | flops 21474836480 | bytes 5242880 | tf_op jit(solution)/shard_map/project_qkv/pallas_call | solution.py:221
  161.2 152.9 %attend_project.1 = bf16[512,2048]{1,0:T(8,128)(2,1)} custom-call(bf16[1024,1024]{1,0:T(8,128)(2,1)} %get-tuple-element.9.q_ref, bf16[4096,256]{1,0:T(8,128)(2,1)} %get-tuple-element.10.kv_ref, s32[8,4,128]{2,1,0:T(4,128)} %get-tuple-element.11.segs_ref, bf16[3,256,2048]{2,1,0:T(8,128)(2,1)} %get-tuple-element.12.got_ref, bf16[1024,2048]{1,0:T(8,128)(2,1)} %w_ref.3), custom_call_target="tpu_custom_call" | custom-call | flops 17179869184 | bytes 8388608 | tf_op jit(solution)/shard_map/attend_project/pallas_call | solution.py:570
  314.1 3.2 copy.6

commit v5 on v4

--- a/solution.py
+++ b/solution.py
@@ -11,7 +11,7 @@
 CORES = 2
 Q_TILE = 256
 CHUNKS = 4
-UNROLL = 2
+UNROLL = 4
 LOG2E = 1.4426950408889634
 BOTH = (0, 1)
 YES, NO = True, False

time: 317 us -> 317 us (level)
  no operation moved by 1% of the time
where the time goes in v5:
time: 317 us
  Pallas kernels  314 us (99%)
    pallas_call x1, Pallas kernels, project_qkv(): pl.pallas_call(functools.partial(qkv_kernel, n_x, n_y), out_shape=(jax.Sh...  161 us
    pallas_call x1, Pallas kernels, attend_project(): pl.pallas_call(functools.partial(attend_kernel, n_x, n_y), out_shape=jax....  153 us

profile of v5, /device:TPU:97, one launch (start us, length us, event | category | flops | bytes accessed | tf_op | source)
XLA Modules:
  0.0 317.3 jit_solution(9977425695020861763)
XLA Ops:
  0.0 161.2 %project_qkv.1 = (bf16[1024,1024]{1,0:T(8,128)(2,1)}, bf16[4096,256]{1,0:T(8,128)(2,1)}, s32[8,4,128]{2,1,0:T(4,128)}, bf16[3,256,2048]{2,1,0:T(8,128)(2,1)}) custom-call(bf16[512,2048]{1,0:T(8,128)(2,1)} %tok_ref.1, bf16[1024,2560]{1,0:T(8,128)(2,1)} %w_ref.2, bf16[1024,2048]{1,0:T(8,128)(2,1)} %w_ref.3, s32[4,128]{1,0:T(4,128)} %bitcast.1), custom_call_target="tpu_custom_call" | custom-call | flops 21474836480 | bytes 5242880 | tf_op jit(solution)/shard_map/project_qkv/pallas_call | solution.py:221
  161.2 152.9 %attend_project.1 = bf16[512,2048]{1,0:T(8,128)(2,1)} custom-call(bf16[1024,1024]{1,0:T(8,128)(2,1)} %get-tuple-element.9.q_ref, bf16[4096,256]{1,0:T(8,128)(2,1)} %get-tuple-element.10.kv_ref, s32[8,4,128]{2,1,0:T(4,128)} %get-tuple-element.11.segs_ref, bf16[3,256,2048]{2,1,0:T(8,128)(2,1)} %get-tuple-element.12.got_ref, bf16[1024,2048]{1,0:T(8,128)(2,1)} %w_ref.3), custom_call_target="tpu_custom_call" | custom-call | flops 17179869184 | bytes 8388608 | tf_op jit(solution)/shard_map/attend_project/pallas_call | solution.py:570
  314.1 3.2 copy.6
